TPU v7x, 128 devices: a whole 4x4x4 slice. The times are simulated.
128 devices in a mesh: mem: 4 (over y_lo, core), lat: 4 (over z), lon: 8 (over y_hi, x).
Axes of the slice: x: 4, y: 4 (y_hi: 2, y_lo: 2; y = y_hi * 2 + y_lo), z: 4, core: 2. Of those that a mesh axis runs over, the one named last changes fastest.
Arguments:
- fields: bfloat16 [4, 2, 96, 384, 512], P('mem', None, 'lat', 'lon'), may hold values from -6 to 6
- region: int32 [96, 384], P('lat', 'lon'), may hold values from 0 to 2
- gain_attn: float32 [512], replicated, may hold values from 0.1 to 1.9
- w_qkv: bfloat16 [512, 1536], P(None, ('mem', 'lat', 'lon')), may hold values from -1 to 1
- w_proj: bfloat16 [512, 512], P(None, ('mem', 'lat', 'lon')), may hold values from -0.25 to 0.25
- gain_mlp: float32 [512], replicated, may hold values from 0.1 to 1.9
- w_up: bfloat16 [512, 2048], P(None, ('mem', 'lat', 'lon')), may hold values from -0.25 to 0.25
- w_down: bfloat16 [2048, 512], P(None, ('mem', 'lat', 'lon')), may hold values from -0.125 to 0.125
Outputs:
- updated: bfloat16 [4, 2, 96, 384, 512], P('mem', None, 'lat', 'lon')
All inputs are finite; a program needn't handle non-finite values.
Results may differ from a plain program's by a relative error of at most 0.011.
Values may be sent and summed in bfloat16 or wider, within the bound.
A program may use at most 192 MiB of HBM per device.

v0:
```python
import jax
import jax.numpy as jnp
from jax import lax
from jax.sharding import PartitionSpec as P

HEADS = 16
HDIM = 32
WLAT = 6
WLON = 12
SH = 3
SL = 6


eps = 1e-05


def in_order(pieces, dim):
    pieces = jnp.moveaxis(pieces, 0, dim)
    shape = pieces.shape
    return pieces.reshape(*shape[:dim], shape[dim] * shape[dim + 1], *shape[dim + 2 :])


def one_gather(arrays, axis, dims):
    flat = jnp.concatenate([a.reshape(-1) for a in arrays])
    lines, at, gathered = (lax.all_gather(flat, axis), 0, [])
    for a, dim in zip(arrays, dims):
        pieces = lines[:, at : at + a.size].reshape(-1, *a.shape)
        gathered.append(in_order(pieces, dim))
        at += a.size
    return tuple(gathered)


def shifted_2(block, axis, distance):
    devices = range(lax.axis_size(axis))
    route = [((i - distance) % len(devices), i) for i in devices]
    return lax.ppermute(block, axis, route)


def layer_norm(values, gain_vec):
    values = values.astype(jnp.float32)
    average = jnp.mean(values, axis=-1, keepdims=True)
    centred = values - average
    variance = jnp.mean(centred * centred, axis=-1, keepdims=True)
    return (centred * lax.rsqrt(variance + eps) * gain_vec).astype(jnp.bfloat16)


def attend(qkv_all, region_ids, north_side, height):
    levels, row_count, col_count, width3 = qkv_all.shape
    width = width3 // 3
    band_count = row_count // height
    win_count = col_count // WLON
    win_tok = levels * height * WLON
    windowed = qkv_all.reshape(levels, band_count, height, win_count, WLON, width3)
    windowed = windowed.transpose(1, 3, 0, 2, 4, 5).reshape(
        band_count * win_count, win_tok, 3, HEADS, width // HEADS
    )
    ids_full = jnp.broadcast_to(region_ids[None], (levels, row_count, col_count))
    ids_full = ids_full.reshape(levels, band_count, height, win_count, WLON).transpose(
        1, 3, 0, 2, 4
    )
    ids_full = ids_full.reshape(band_count * win_count, win_tok)
    north_full = jnp.broadcast_to(north_side[None, :, None], (levels, row_count, col_count))
    north_full = north_full.reshape(levels, band_count, height, win_count, WLON).transpose(
        1, 3, 0, 2, 4
    )
    north_full = north_full.reshape(band_count * win_count, win_tok)
    scores = jnp.einsum(
        "wqhd,wkhd->whqk", windowed[:, :, 0], windowed[:, :, 1], preferred_element_type=jnp.float32
    )
    scores = scores * (1.0 / HDIM**0.5)
    allow = (ids_full[:, :, None] == ids_full[:, None, :]) & (
        north_full[:, :, None] == north_full[:, None, :]
    )
    scores = jnp.where(allow[:, None], scores, -1000000000.0)
    attn_probs = jax.nn.softmax(scores, axis=-1).astype(jnp.bfloat16)
    mixed_heads = jnp.einsum(
        "whqk,wkhd->wqhd", attn_probs, windowed[:, :, 2], preferred_element_type=jnp.float32
    )
    mixed_heads = mixed_heads.astype(jnp.bfloat16).reshape(
        band_count, win_count, levels, height, WLON, width
    )
    return mixed_heads.transpose(2, 0, 3, 1, 4, 5).reshape(levels, row_count, col_count, width)


def body(fields, region, gain_attn, w_qkv, w_proj, gain_mlp, w_up, w_down):
    gathered = one_gather((w_qkv, w_proj, w_up, w_down), ("mem", "lat", "lon"), (1, 1, 1, 1))
    member = fields[0]
    levels, clat, clon, width = member.shape
    normed = layer_norm(member, gain_attn)
    region_ids = region.astype(jnp.bfloat16)
    lat_pos = lax.axis_index("lat")
    nlat_all = clat * lax.axis_size("lat")
    row_ids = jnp.arange(clat, dtype=jnp.int32)
    north_side = (lat_pos * clat + SH + row_ids) % nlat_all < SH
    arrived, arrived_ids = shifted_2((normed[:, :SH], region_ids[:SH]), "lat", -1)
    lat_band = jnp.concatenate([normed[:, SH:], arrived], axis=1)
    band_ids = jnp.concatenate([region_ids[SH:], arrived_ids], axis=0)
    strip, strip_ids = shifted_2((lat_band[:, :, :SL], band_ids[:, :SL]), "lon", -1)
    shifted = jnp.concatenate([lat_band[:, :, SL:], strip], axis=2)
    shifted_ids = jnp.concatenate([band_ids[:, SL:], strip_ids], axis=1)
    qkv_all = (
        jnp.dot(shifted.reshape(-1, width), gathered[0], preferred_element_type=jnp.float32)
        .astype(jnp.bfloat16)
        .reshape(levels, clat, clon, 3 * width)
    )
    mixed_heads = attend(qkv_all, shifted_ids, north_side, WLAT)
    attn_out = (
        jnp.dot(mixed_heads.reshape(-1, width), gathered[1], preferred_element_type=jnp.float32)
        .astype(jnp.bfloat16)
        .reshape(levels, clat, clon, width)
    )
    arrived_cols = shifted_2(attn_out[:, :, clon - SL :], "lon", 1)
    attn_out = jnp.concatenate([arrived_cols, attn_out[:, :, : clon - SL]], axis=2)
    arrived_rows = shifted_2(attn_out[:, clat - SH :], "lat", 1)
    attn_out = jnp.concatenate([arrived_rows, attn_out[:, : clat - SH]], axis=1)
    resid = (member.astype(jnp.float32) + attn_out.astype(jnp.float32)).astype(jnp.bfloat16)
    normed2 = layer_norm(resid, gain_mlp).reshape(-1, width)
    pre_act = jnp.dot(normed2, gathered[2], preferred_element_type=jnp.float32)
    hidden = jax.nn.gelu(pre_act, approximate=False).astype(jnp.bfloat16)
    delta = jnp.dot(hidden, gathered[3], preferred_element_type=jnp.float32).reshape(
        levels, clat, clon, width
    )
    updated = (resid.astype(jnp.float32) + delta).astype(jnp.bfloat16)
    return updated[None]


def solution(mesh):
    in_specs = (
        P("mem", None, "lat", "lon", None),
        P("lat", "lon"),
        P(),
        P(None, ("mem", "lat", "lon")),
        P(None, ("mem", "lat", "lon")),
        P(),
        P(None, ("mem", "lat", "lon")),
        P(None, ("mem", "lat", "lon")),
    )
    out_specs = P("mem", None, "lat", "lon", None)
    return jax.shard_map(body, mesh=mesh, in_specs=in_specs, out_specs=out_specs, check_vma=False)
```

profile of v0, /device:TPU:1, one launch (start us, length us, event | category | flops | bytes accessed | tf_op | source)
XLA Modules:
  0.0 644.1 jit_solution(7595094467053468557)
XLA Ops:
  6.5 1.0 copy.49
  7.6 0.2 reshape.154
  7.8 0.9 copy.50
  8.6 0.2 reshape.155
  8.8 0.8 copy.51
  9.8 1.0 copy.52
  10.8 0.8 reshape.157
  11.6 0.6 pad_maximum_fusion.4
  12.3 0.7 convert_element_type.75
  13.0 4.6 collective-permute-start.2
  17.6 2.0 convert_reduce_fusion.1
  19.7 1.0 fusion.22
  20.7 0.9 fusion.24
  21.7 1.4 copy-done.3
  23.1 0.2 collective-permute-start
  23.3 1.7 slice.76
  25.3 5.2 collective-permute-start.3
  30.5 0.7 collective-permute-done.3
  31.7 5.4 collective-permute-start.1
  37.1 0.9 compare_and_fusion
  38.0 0.6 slice_maximum_fusion
  38.7 4.6 collective-permute-done.1
  43.3 1.8 pad_maximum_fusion
  45.0 276.8 %all-gather.3.cloned.1.call-done = bf16[3145728]{0:T(1024)(128)(2,1)} async-done(((bf16[24576]{0:T(1024)(128)(2,1)}), bf16[3145728]{0:T(1024)(128)(2,1)}) %all-gather.3.cloned.1.call-update) | async-done | bytes 6291472 | tf_op jit(solution)/shard_map/all_gather | solution.py:25
  321.8 8.8 %reshape.169 = bf16[128,24576]{1,0:T(8,128)(2,1)} reshape(bf16[3145728]{0:T(1024)(128)(2,1)} %all-gather.3.cloned.1.call-done) | data formatting | bytes 12582912 | tf_op jit(solution)/shard_map/all_gather | solution.py:25
  330.6 1.2 slice.88
  331.8 0.3 copy.63
  332.1 0.5 copy.64
  332.7 0.9 reshape.163
  333.6 1.6 copy.53
  335.2 2.3 reshape.158
  337.5 3.6 copy.54
  341.1 2.5 reshape.159
  343.6 7.6 %convolution_convert_fusion = bf16[2304,1536]{1,0:T(8,128)(2,1)} fusion(bf16[2304,512]{1,0:T(8,128)(2,1)} %bitcast.115, bf16[512,1536]{0,1:T(8,128)(2,1)S(1)} %reshape.159), kind=kOutput, calls=%fused_computation.29 | convolution fusion | flops 3627417600 | bytes 11010048 | tf_op jit(solution)/shard_map/dot_general | solution.py:102
  351.2 11.3 %reshape_reshape.6 = bf16[2,4,6,4,12,1536]{5,4,3,2,1,0:T(8,128)(2,1)} reshape(bf16[2304,1536]{1,0:T(8,128)(2,1)} %convolution_convert_fusion) | data formatting | bytes 14155776 | tf_op jit(solution)/shard_map/reshape;reshape | solution.py:53
  362.5 12.0 %copy.55 = bf16[4,4,2,6,12,1536]{5,1,0,4,3,2:T(4,128)(2,1)} copy(bf16[4,4,2,6,12,1536]{5,4,1,3,0,2:T(8,128)(2,1)} %bitcast.103) | data formatting | bytes 14155776 | tf_op jit(solution)/shard_map/transpose | solution.py:54
  374.5 32.6 %reshape.160 = bf16[16,144,3,16,32]{4,3,2,0,1:T(8,128)(2,1)} reshape(bf16[4,4,2,6,12,1536]{5,1,0,4,3,2:T(4,128)(2,1)} %copy.55) | data formatting | bytes 14155776 | tf_op jit(solution)/shard_map/reshape | solution.py:54
  407.1 24.0 %fusion.52 = (bf16[16,144,1,16,32]{4,3,2,0,1:T(8,128)(2,1)}, bf16[16,144,1,16,32]{4,3,2,0,1:T(8,128)(2,1)}, bf16[16,144,1,16,32]{4,3,2,0,1:T(8,128)(2,1)}) fusion(bf16[16,144,3,16,32]{4,3,2,0,1:T(8,128)(2,1)} %reshape.160), kind=kLoop, calls=%fused_computation.82 | loop fusion | bytes 14155776 | tf_op jit(solution)/shard_map/slice | solution.py:77
  431.1 12.3 %copy.73 = bf16[16,144,1,16,32]{1,4,3,0,2:T(8,128)(2,1)} copy(bf16[16,144,1,16,32]{4,3,2,0,1:T(8,128)(2,1)} %get-tuple-element.5) | data formatting | bytes 4718592
  443.4 12.3 %copy.74 = bf16[16,144,1,16,32]{1,4,3,0,2:T(8,128)(2,1)} copy(bf16[16,144,1,16,32]{4,3,2,0,1:T(8,128)(2,1)} %get-tuple-element.6) | data formatting | bytes 4718592
  455.7 12.3 %copy.75 = bf16[16,144,1,16,32]{1,4,3,0,2:T(8,128)(2,1)} copy(bf16[16,144,1,16,32]{4,3,2,0,1:T(8,128)(2,1)} %get-tuple-element.7) | data formatting | bytes 4718592
  468.0 19.9 %fusion.54 = (f32[16,16,144]{2,1,0:T(8,128)S(1)}, f32[16,16,144,144]{2,3,1,0:T(8,128)}) fusion(pred[16,144,144]{1,2,0:T(8,128)(4,1)S(1)} %compare_and_fusion, bf16[16,144,1,16,32]{1,4,3,0,2:T(8,128)(2,1)} %copy.75, bf16[16,144,1,16,32]{1,4,3,0,2:T(8,128)(2,1)} %copy.74), kind=kOutput, calls=%fused_computation.84 | convolution fusion | flops 360972416 | bytes 26431488 | tf_op jit(solution)/shard_map/sub | solution.py:75
  487.8 16.4 %convert_bitcast_fusion.1 = bf16[16,144,16,32]{1,3,2,0:T(8,128)(2,1)} fusion(f32[16,16,144,144]{2,3,1,0:T(8,128)} %get-tuple-element.11, f32[16,16,144]{2,1,0:T(8,128)S(1)} %get-tuple-element.10, bf16[16,144,1,16,32]{1,4,3,0,2:T(8,128)(2,1)} %copy.73), kind=kOutput, calls=%fused_computation.56 | convolution fusion | flops 351535104 | bytes 26099712 | tf_op jit(solution)/shard_map/whqk,wkhd->wqhd/dot_general | solution.py:76
  504.3 11.5 %copy.61 = bf16[16,144,16,32]{3,2,0,1:T(8,128)(2,1)} copy(bf16[16,144,16,32]{1,3,2,0:T(8,128)(2,1)} %convert_bitcast_fusion.1) | data formatting | bytes 4718592 | tf_op jit(solution)/shard_map/convert_element_type | solution.py:79
  515.8 12.2 %reshape.161 = bf16[4,4,2,6,12,512]{5,1,0,4,3,2:T(4,128)(2,1)S(1)} reshape(bf16[16,144,16,32]{3,2,0,1:T(8,128)(2,1)} %copy.61) | data formatting | bytes 4718592 | tf_op jit(solution)/shard_map/reshape | solution.py:79
  528.0 3.8 copy.62
  531.8 5.1 reshape_reshape.7
  536.9 3.2 convolution_convert_fusion.1
  540.3 1.9 collective-permute-start.4
  542.1 12.5 %collective-permute-done.4 = bf16[2,24,6,512]{3,2,1,0:T(8,128)(2,1)S(1)} collective-permute-done((bf16[2,24,6,512]{3,2,1,0:T(8,128)(2,1)S(1)}, bf16[2,24,6,512]{3,2,1,0:T(8,128)(2,1)S(1)}, u32[]{:S(2)}, u32[]{:S(2)}) %collective-permute-start.4) | collective-permute-done | bytes 294944 | tf_op jit(solution)/shard_map/ppermute | solution.py:36
  554.7 1.6 collective-permute-start.5
  556.3 2.2 fusion.53
  558.5 3.2 copy.67
  561.7 4.0 copy.68
  565.7 4.1 reshape.168
  569.8 2.4 copy.65
  572.3 5.1 copy.66
  577.4 2.8 pad_maximum_fusion.1
  580.2 0.7 convert_reduce_fusion
  580.9 1.3 fusion.28
  582.3 1.1 multiply_convert_fusion
  583.4 0.4 copy-done.6
  583.8 45.8 %fusion.4 = bf16[2304,2048]{1,0:T(8,128)(2,1)S(1)} fusion(bf16[2304,512]{1,0:T(8,128)(2,1)S(1)} %bitcast.116, bf16[512,2048]{0,1:T(8,128)(2,1)S(1)} %bitcast.117), kind=kOutput, calls=%fused_computation.8 | convolution fusion | flops 5138546688 | bytes 13893632 | tf_op jit(solution)/shard_map/dot_general | solution.py:118
  629.6 7.2 %fusion.44 = bf16[1,2,24,48,512]{4,3,2,1,0:T(8,128)(2,1)} fusion(bf16[2,24,48,2048]{3,2,1,0:T(8,128)(2,1)S(1)} %bitcast.119, bf16[2048,512]{0,1:T(8,128)(2,1)S(1)} %copy-done.5, bf16[2,21,48,512]{3,2,1,0:T(8,128)(2,1)S(1)} %pad_maximum_fusion.1, bf16[2,3,48,512]{3,2,1,0:T(8,128)(2,1)S(1)} %collective-permute-done.5, ...), kind=kOutput, calls=%fused_computation.57 | convolution fusion | flops 4841275392 | bytes 18612224 | tf_op jit(solution)/shard_map/dot_general | solution.py:120
  (51 shorter events, 1.2 us)
Async XLA Ops:
  6.5 13.1 %copy-start = (bf16[1,2,24,48,512]{4,3,2,1,0:T(8,128)(2,1)S(1)}, bf16[1,2,24,48,512]{4,3,2,1,0:T(8,128)(2,1)}, u32[]{:S(2)}) copy-start(bf16[1,2,24,48,512]{4,3,2,1,0:T(8,128)(2,1)} %param.8) | copy-start | bytes 7077892
  6.5 14.2 %copy-start.8 = (f32[512]{0:T(512)S(1)}, f32[512]{0:T(512)}, u32[]{:S(2)}) copy-start(f32[512]{0:T(512)} %param.10) | copy-start | bytes 6148
  6.5 315.3 %all-gather.3.cloned.1.call-start = ((), (), s32[]{:S(2)}) async-start(), calls=%async_computation | async-start | bytes 6340608 | tf_op jit(solution)/shard_map/all_gather | solution.py:25
  13.0 12.2 %collective-permute-start.2 = (bf16[3,48]{1,0:T(4,128)(2,1)S(1)}, bf16[3,48]{1,0:T(4,128)(2,1)S(1)}, u32[]{:S(2)}, u32[]{:S(2)}) collective-permute-start(bf16[3,48]{1,0:T(4,128)(2,1)S(1)} %slice.83), channel_id=1, source_target_pairs={{8,0},{16,8},{24,16},{0,24},{9,1},{17,9},{25,17},{1,25},{10,2},{18... | collective-permute-start | bytes 872 | tf_op jit(solution)/shard_map/ppermute | solution.py:36
  21.7 1.4 copy-start.3
  23.1 8.6 %collective-permute-start = (bf16[2,3,48,512]{3,2,1,0:T(8,128)(2,1)S(1)}, bf16[2,3,48,512]{3,2,1,0:T(8,128)(2,1)S(1)}, u32[]{:S(2)}, u32[]{:S(2)}) collective-permute-start(bf16[2,3,48,512]{3,2,1,0:T(8,128)(2,1)S(1)} %slice.77), channel_id=1, source_target_pairs={{8,0},{16,8},{24,16},{0,24},{9,1},{17,9},{25,17},{1,25},{10,2},{18... | collective-permute-start | bytes 884744 | tf_op jit(solution)/shard_map/ppermute | solution.py:36
  25.3 6.0 collective-permute-start.3
  31.7 11.5 %collective-permute-start.1 = (bf16[2,24,6,512]{3,2,1,0:T(8,128)(2,1)S(1)}, bf16[2,24,6,512]{3,2,1,0:T(8,128)(2,1)S(1)}, u32[]{:S(2)}, u32[]{:S(2)}) collective-permute-start(bf16[2,24,6,512]{3,2,1,0:T(8,128)(2,1)S(1)} %pad_maximum_fusion.2), channel_id=1, source_target_pairs={{1,0},{2,1},{3,2},{4,3},{5,4},{6,5},{7,6},{0,7},{9,8},{10,9},{11,1... | collective-permute-start | bytes 884744 | tf_op jit(solution)/shard_map/ppermute | solution.py:36
  330.6 3.0 slice-start.2
  528.0 8.9 %copy-start.7 = (bf16[512,512]{0,1:T(8,128)(2,1)S(1)}, bf16[512,512]{0,1:T(8,128)(2,1)}, u32[]{:S(2)}) copy-start(bf16[512,512]{0,1:T(8,128)(2,1)} %reshape.163) | copy-start | bytes 1572868
  531.8 24.5 %slice-start = ((s8[6291456]{0:T(1024)(128)(4,1)}), s8[2097152]{0:T(1024)(128)(4,1)S(1)}, s32[]{:S(2)}) async-start(s8[6291456]{0:T(1024)(128)(4,1)} %bitcast.105), calls=%async_computation.1 | async-start | bytes 4194304
  536.9 19.4 %slice-start.1 = ((s8[6291456]{0:T(1024)(128)(4,1)}), s8[4194304]{0:T(1024)(128)(4,1)S(1)}, s32[]{:S(2)}) async-start(s8[6291456]{0:T(1024)(128)(4,1)} %bitcast.105), calls=%async_computation.2 | async-start | bytes 8388608
  540.1 14.5 %copy-start.2 = (bf16[2304,512]{1,0:T(8,128)(2,1)}, bf16[2304,512]{1,0:T(8,128)(2,1)S(1)}, u32[]{:S(2)}) copy-start(bf16[2304,512]{1,0:T(8,128)(2,1)S(1)} %convolution_convert_fusion.1) | copy-start | bytes 7077892
  540.3 14.3 %collective-permute-start.4 = (bf16[2,24,6,512]{3,2,1,0:T(8,128)(2,1)S(1)}, bf16[2,24,6,512]{3,2,1,0:T(8,128)(2,1)S(1)}, u32[]{:S(2)}, u32[]{:S(2)}) collective-permute-start(bf16[2,24,6,512]{3,2,1,0:T(8,128)(2,1)S(1)} %slice.89), channel_id=1, source_target_pairs={{7,0},{0,1},{1,2},{2,3},{3,4},{4,5},{5,6},{6,7},{15,8},{8,9},{9,10... | collective-permute-start | bytes 884744 | tf_op jit(solution)/shard_map/ppermute | solution.py:36
  554.7 25.4 %collective-permute-start.5 = (bf16[2,3,48,512]{3,2,1,0:T(8,128)(2,1)S(1)}, bf16[2,3,48,512]{3,2,1,0:T(8,128)(2,1)S(1)}, u32[]{:S(2)}, u32[]{:S(2)}) collective-permute-start(bf16[2,3,48,512]{3,2,1,0:T(8,128)(2,1)S(1)} %pad_maximum_fusion.3), channel_id=1, source_target_pairs={{24,0},{0,8},{8,16},{16,24},{25,1},{1,9},{9,17},{17,25},{26,2},{2,... | collective-permute-start | bytes 884744 | tf_op jit(solution)/shard_map/ppermute | solution.py:36
  565.7 4.1 copy-start.4
  572.3 7.9 %copy-start.1 = (bf16[1,2,24,48,512]{4,3,2,1,0:T(8,128)(2,1)S(1)}, bf16[1,2,24,48,512]{4,3,2,1,0:T(8,128)(2,1)}, u32[]{:S(2)}) copy-start(bf16[1,2,24,48,512]{4,3,2,1,0:T(8,128)(2,1)} %param.8) | copy-start | bytes 7077892
  580.1 2.1 copy-start.9
  582.2 1.6 copy-start.6
  583.8 45.8 %copy-start.5 = (bf16[2048,512]{0,1:T(8,128)(2,1)S(1)}, bf16[2048,512]{0,1:T(8,128)(2,1)}, u32[]{:S(2)}) copy-start(bf16[2048,512]{0,1:T(8,128)(2,1)} %reshape.168) | copy-start | bytes 6291460
Sparse Core Ops, SparseCore 0:
  12.4 309.3 all-gather.2
where the time goes:
time: 652 us; the launch traced here: 644 us
  waiting for transfers between devices  295 us (45%)
  local copies, waits for them, and re-layouts  201 us (31%)
  matrix products  100 us (15%)
  starting transfers between devices  18.8 us (3%)
  other arithmetic  14.9 us (2%)
  between operations  14.2 us (2%)
    all_gather x1, waiting for transfers between devices, one_gather(): lines, at, gathered = (lax.all_gather(flat, axis), 0, [])  277 us
    dot_general x1, matrix products, body(): pre_act = jnp.dot(normed2, gathered[2], preferred_element_type=jnp.float32)  45.8 us
    unnamed x31, local copies, waits for them, and re-layouts  42.4 us
    reshape x1, local copies, waits for them, and re-layouts, attend(): windowed.transpose(1, 3, 0, 2, 4, 5)  32.6 us
    slice x1, local copies, waits for them, and re-layouts, attend(): windowed[:, :, 2]  24 us
    sub x1, matrix products, attend(): attn_probs = jax.nn.softmax(scores, axis=-1).astype(jnp.bfloat16)  19.9 us
    ppermute x6, starting transfers between devices, shifted_2(): return lax.ppermute(block, axis, route)  18.8 us
    ppermute x6, waiting for transfers between devices, shifted_2(): return lax.ppermute(block, axis, route)  18 us
  transfers between devices with their start and end apart: 7, of which 5 were waited for; matrix products, arithmetic and copies ran while one was open for 5% of the time, Pallas kernels for 0%

commit v1 on v0

v1 whole, which is shorter than its diff:
```python
import functools

import jax
import jax.numpy as jnp
from jax import lax
from jax.experimental import pallas as pl
from jax.experimental.pallas import tpu as pltpu
from jax.sharding import PartitionSpec as P

D = 512
FF = 2048
HDIM = 32
WLAT = 6
WLON = 12
WTOK = 144
SH = 3
SL = 6
NLAT_ALL = 96
QSCALE = 1.4426950408889634 / HDIM**0.5
NEG = -1e30
EPS = 1e-05
MESH = pl.DeviceIdType.MESH
BF = jnp.bfloat16
F32 = jnp.float32

S_P1 = 0
S_P2 = 3
S_UP = 6
S_DN = 10
S_FW = 14
S_CO = 18
S_ALL = 34


def nt(a, b):
    return lax.dot_general(a, b, (((1,), (1,)), ((), ())), preferred_element_type=F32)


def nn(a, b):
    return lax.dot_general(a, b, (((1,), (0,)), ((), ())), preferred_element_type=F32)


def norm(x, gain):
    x = x.astype(F32)
    mean = jnp.mean(x, axis=-1, keepdims=True)
    cen = x - mean
    var = jnp.mean(cen * cen, axis=-1, keepdims=True)
    return (cen * lax.rsqrt(var + EPS) * gain).astype(BF)


def kernel(
    shard,
    fields,
    region,
    gain_a,
    gain_m,
    toks,
    out,
    gat,
    fx,
    reg,
    w_qkv,
    w_p,
    w_d,
    xb,
    q_s,
    k_s,
    vt_s,
    mt,
    mix,
    ox,
    ic,
    km_mask,
    tq_mask,
    to_mask,
    ob,
    send,
    recv,
    loc,
    hsend,
    hrecv,
    osem,
):
    mem = lax.axis_index("mem")
    lat = lax.axis_index("lat")
    lon = lax.axis_index("lon")
    core = mem % 2
    y_lo = mem // 2
    y_hi = lon // 4
    x0 = lon % 4
    y0 = y_hi * 2 + y_lo
    pos = (x0, y0, lat)

    def dev(x, y, z, c):
        return ((y % 2) * 2 + c, z, (y // 2) * 4 + x)

    def moved(axis, dist, c=None):
        p = list(pos)
        p[axis] = (p[axis] + dist) % 4
        return dev(*p, core if c is None else c)

    sibling = dev(*pos, 1 - core)
    lat_b, lat_f = (lat + 3) % 4, (lat + 1) % 4
    lon_b, lon_f = (lon + 7) % 8, (lon + 1) % 8

    bar = pltpu.get_barrier_semaphore()
    peers = [moved(a, d) for a in range(3) for d in (1, 2, 3)] + [sibling]
    peers += [(mem, lat, lon_b), (mem, lat, lon_f), (mem, lat_b, lon_b), (mem, lat_f, lon_f)]
    for d in peers:
        pl.semaphore_signal(bar, inc=1, device_id=d, device_id_type=MESH)

    own = pltpu.make_async_copy(fields, fx.at[:, pl.ds(0, 24), pl.ds(0, 48)], loc.at[3])
    own.start()
    own_reg = pltpu.make_async_copy(region, reg.at[0, pl.ds(0, 24)], loc.at[4])
    own_reg.start()

    def chip(x, y, z, c):
        return (y % 2, c, z, y // 2, x)

    locals_ = []
    for p in range(3):
        cp = pltpu.make_async_copy(shard.at[p], gat.at[(p, *chip(*pos, core))], loc.at[p])
        cp.start()
        locals_.append(cp)

    pl.semaphore_wait(bar, len(peers))

    def remote(src, dst, s, r, d):
        cp = pltpu.make_async_remote_copy(
            src_ref=src, dst_ref=dst, send_sem=s, recv_sem=r, device_id=d, device_id_type=MESH
        )
        cp.start()
        return cp

    pend = []

    def blk(p, bval, cval, c):
        a, b, cc = p, (p + 1) % 3, (p + 2) % 3
        v = [None, None, None]
        v[b], v[cc] = bval, cval
        x, y, z = v
        full = pl.ds(0, 4)
        if y is None:
            yl, yh = pl.ds(0, 2), pl.ds(0, 2)
        else:
            yl, yh = y % 2, y // 2
        x = full if x is None else x
        z = full if z is None else z
        return gat.at[p, yl, c, z, yh, x]

    ph1 = {}
    for p in range(3):
        for i, d in enumerate((1, 3, 2)):
            here = gat.at[(p, *chip(*pos, core))]
            ph1[p, i] = remote(
                shard.at[p], here, send.at[p, S_P1 + i], recv.at[p, S_P1 + i], moved(p, d)
            )
            pend.append(ph1[p, i])

    halos = []
    fsl = (
        (fields.at[:, pl.ds(0, 3)], fx.at[:, pl.ds(24, 3), pl.ds(0, 48)], (mem, lat_b, lon)),
        (fields.at[:, :, pl.ds(0, 8)], fx.at[:, pl.ds(0, 24), pl.ds(48, 8)], (mem, lat, lon_b)),
        (
            fields.at[:, pl.ds(0, 3), pl.ds(0, 8)],
            fx.at[:, pl.ds(24, 3), pl.ds(48, 8)],
            (mem, lat_b, lon_b),
        ),
        (region, reg.at[0, pl.ds(24, 24)], (mem, lat_b, lon)),
        (region, reg.at[1, pl.ds(0, 24)], (mem, lat, lon_b)),
        (region, reg.at[1, pl.ds(24, 24)], (mem, lat_b, lon_b)),
    )
    for i, (s, t, d) in enumerate(fsl):
        halos.append(remote(s, t, hsend.at[i], hrecv.at[i], d))

    for cp in locals_:
        cp.wait()

    b0 = [pos[(p + 1) % 3] for p in range(3)]
    c0 = [pos[(p + 2) % 3] for p in range(3)]
    ph2, up, down, fwd, swap = {}, {}, {}, {}, {}
    dists = (0, 3, 1, 2)

    def to_core(p, slot, bval, cval):
        r = blk(p, bval, cval, core)
        swap[p, slot] = remote(r, r, send.at[p, S_CO + slot], recv.at[p, S_CO + slot], sibling)
        pend.append(swap[p, slot])

    def to_last(p, i):
        bval = (b0[p] + dists[i]) % 4
        r = blk(p, bval, c0[p], core)
        ax = (p + 2) % 3
        up[p, i] = remote(r, r, send.at[p, S_UP + i], recv.at[p, S_UP + i], moved(ax, 1))
        down[p, i] = remote(r, r, send.at[p, S_DN + i], recv.at[p, S_DN + i], moved(ax, 3))
        pend.extend((up[p, i], down[p, i]))
        to_core(p, i, bval, c0[p])

    for p in range(3):
        for i in range(3):
            ph1[p, i].wait_recv()
        r = blk(p, b0[p], c0[p], core)
        for i, d in enumerate((1, 3, 2)):
            ph2[p, i] = remote(
                r, r, send.at[p, S_P2 + i], recv.at[p, S_P2 + i], moved((p + 1) % 3, d)
            )
            pend.append(ph2[p, i])
        to_last(p, 0)
    for i in range(3):
        for p in range(3):
            ph2[p, i].wait_recv()
            to_last(p, i + 1)

    lane = lax.broadcasted_iota(jnp.int32, (WTOK, 128), 1)
    for h in range(4):
        km_mask[h] = jnp.where((lane >> 5) == h, 1.0, 0.0).astype(BF)
    tr = lax.broadcasted_iota(jnp.int32, (128, 256), 0)
    tl = lax.broadcasted_iota(jnp.int32, (128, 256), 1)
    tq_mask[...] = jnp.where((tr >> 4) == (tl >> 5), 1.0, 0.0).astype(BF)
    tr = lax.broadcasted_iota(jnp.int32, (256, 128), 0)
    tl = lax.broadcasted_iota(jnp.int32, (256, 128), 1)
    to_mask[...] = jnp.where((tr >> 5) == (tl >> 4), 1.0, 0.0)

    is_up = core == 0
    for i in range(4):
        for p in range(3):
            bval = (b0[p] + dists[i]) % 4
            ax = (p + 2) % 3
            up[p, i].wait_recv()
            down[p, i].wait_recv()
            cval = jnp.where(is_up, (c0[p] + 3) % 4, (c0[p] + 1) % 4)
            step = jnp.where(is_up, 1, 3)
            r = blk(p, bval, cval, core)
            fwd[p, i] = remote(
                r, r, send.at[p, S_FW + i], recv.at[p, S_FW + i], moved(ax, step)
            )
            pend.append(fwd[p, i])
            to_core(p, 4 + i, bval, (c0[p] + 3) % 4)
            to_core(p, 8 + i, bval, (c0[p] + 1) % 4)
    for i in range(4):
        for p in range(3):
            bval = (b0[p] + dists[i]) % 4
            fwd[p, i].wait_recv()
            to_core(p, 12 + i, bval, (c0[p] + 2) % 4)
    for p in range(3):
        for i in range(16):
            swap[p, i].wait_recv()
    own.wait()
    own_reg.wait()
    for h in halos:
        h.wait_recv()

    @pl.loop(0, 32)
    def _(g):
        at = (g // 16, (g // 8) % 2, (g // 2) % 4, g % 2)
        v = gat[(0, *at)]
        w_qkv[pl.ds(pl.multiple_of(g * 48, 16), 48), :] = jnp.concatenate(
            [v[i, 0:12] for i in range(4)], axis=0
        )
        w_p[pl.ds(pl.multiple_of(g * 16, 16), 16), :] = jnp.concatenate(
            [v[i, 12:16] for i in range(4)], axis=0
        )
        u = gat[(2, *at)]
        for k in range(4):
            w_d[pl.ds(pl.multiple_of(g * 16, 16), 16), 512 * k : 512 * k + 512] = jnp.concatenate(
                [u[i, 4 * k : 4 * k + 4] for i in range(4)], axis=0
            )

    @pl.loop(0, 4)
    def _(b):
        for w in range(4):
            pieces = [
                fx[l, 6 * b + SH + i, WLON * w + SL : WLON * w + SL + WLON, :]
                for l in range(2)
                for i in range(WLAT)
            ]
            xw = norm(jnp.concatenate(pieces, axis=0), gain_a[...])
            xb[WTOK * w : WTOK * w + WTOK, :] = xw
        rows = pl.ds(pl.multiple_of(b * 576, 16), 576)
        for n in range(2):
            cols = slice(256 * n, 256 * n + 256)
            q = nt(xb[...], w_qkv[256 * n : 256 * n + 256, :])
            q_s[rows, cols] = (q * QSCALE).astype(BF)
            k = nt(xb[...], w_qkv[512 + 256 * n : 512 + 256 * n + 256, :])
            k_s[rows, cols] = k.astype(BF)
        for w in range(4):
            vt = nt(w_qkv[1024:1536, :], xb[WTOK * w : WTOK * w + WTOK, :])
            vt_s[b * 4 + w] = vt.astype(BF)

    def window(b, w):
        win = b * 4 + w
        rows = pl.ds(pl.multiple_of(win * WTOK, 16), WTOK)
        row = toks[0] + (6 * b + SH)
        col = toks[1] + (WLON * w + SL)
        l48 = lax.broadcasted_iota(jnp.int32, (WTOK, 48), 1)
        sel = jnp.where(l48 == row, 1.0, 0.0).astype(BF)
        near = nn(sel, reg[0].astype(F32).astype(BF))
        far = nn(sel, reg[1].astype(F32).astype(BF))
        ids = jnp.sum(
            jnp.where(l48 == col, near, 0.0) + jnp.where(l48 + 48 == col, far, 0.0),
            axis=1,
            keepdims=True,
        )
        glob = lat * 24 + row
        glob = jnp.where(glob >= NLAT_ALL, glob - NLAT_ALL, glob)
        code = ids * 2.0 + jnp.where(glob < SH, 1.0, 0.0)
        hot = jnp.where(code == lane.astype(F32), 1.0, 0.0).astype(BF)
        bias_m = (nt(hot, hot[0:128]) - 1.0) * (-NEG)
        bias_t = (nt(hot, jnp.concatenate([hot[128:144]] * 8, axis=0)) - 1.0) * (-NEG)

        def softmax(s):
            m = jnp.max(s, axis=0, keepdims=True)
            e = jnp.exp2(s - m)
            return e.astype(BF), 1.0 / jnp.sum(e, axis=0, keepdims=True)

        for g in range(2):
            for s in range(2):
                at = 256 * g + 128 * s
                k4 = k_s[rows, at : at + 128]
                q4 = q_s[pl.ds(pl.multiple_of(win * WTOK, 16), 128), at : at + 128]
                for h in range(4):
                    e, inv = softmax(nt(k4 * km_mask[h], q4) + bias_m)
                    o = nn(vt_s[win, at + 32 * h : at + 32 * h + 32, :], e)
                    mt[at + 32 * h : at + 32 * h + 32, :] = (o * inv).astype(BF)
            at = 256 * g
            qt = q_s[pl.ds(pl.multiple_of(win * WTOK + 128, 16), 16), at : at + 256]
            qt = jnp.concatenate([qt] * 8, axis=0) * tq_mask[...]
            e, inv = softmax(nt(k_s[rows, at : at + 256], qt) + bias_t)
            o = nn(vt_s[win, at : at + 256, :], e)
            o = (o * inv * to_mask[...]).astype(BF).T
            acc = o[0:16]
            for h in range(1, 8):
                acc = acc + o[16 * h : 16 * h + 16]
            mix[pl.ds(pl.multiple_of(w * WTOK + 128, 16), 16), at : at + 256] = acc
        mix[pl.ds(pl.multiple_of(w * WTOK, 16), 128), :] = mt[...].T

    zeros = jnp.zeros((8, D), BF)

    @pl.loop(0, 4)
    def _(b):
        @pl.loop(0, 4)
        def _(w):
            window(b, w)

        ao = nt(mix[...], w_p[...]).astype(BF)
        for l in range(2):
            for i in range(WLAT):
                at = 72 * l + 12 * i
                pieces = [ao[WTOK * w + at : WTOK * w + at + 12] for w in range(4)]
                ox[l, 6 * b + SH + i] = jnp.concatenate(
                    [zeros[0:6], *pieces, zeros[0:2]], axis=0
                )

    backs = []
    bsl = (
        (ox.at[:, pl.ds(3, 21), pl.ds(48, 8)], ic.at[:, pl.ds(3, 21)], (mem, lat, lon_f)),
        (ox.at[:, pl.ds(24, 3), pl.ds(0, 48)], ox.at[:, pl.ds(0, 3), pl.ds(0, 48)], (mem, lat_f, lon)),
        (ox.at[:, pl.ds(24, 3), pl.ds(48, 8)], ic.at[:, pl.ds(0, 3)], (mem, lat_f, lon_f)),
    )
    for i, (s, t, d) in enumerate(bsl):
        backs.append(remote(s, t, hsend.at[6 + i], hrecv.at[6 + i], d))
    for cp in backs:
        cp.wait_recv()

    first = lax.broadcasted_iota(jnp.int32, (12, 8, D), 1) < SL

    outs = []
    for t in range(4):
        l, r = t // 2, 12 * (t % 2)
        att = ox[l, r : r + 12, 0:48, :].astype(F32)
        head = jnp.where(first, ic[l, r : r + 12].astype(F32), att[:, 0:8])
        att = jnp.concatenate([head, att[:, 8:48]], axis=1)
        res = (fx[l, r : r + 12, 0:48, :].astype(F32) + att).astype(BF).reshape(576, D)
        xb[...] = norm(res, gain_m[...])
        acc = res.astype(F32)
        for k in range(4):
            pre = nt(xb[...], gat[1, k // 2, k % 2].reshape(512, D))
            hid = (0.5 * pre * (1.0 + lax.erf(pre * 0.7071067811865476))).astype(BF)
            acc = acc + nt(hid, w_d[:, 512 * k : 512 * k + 512])
        ob[t] = acc.astype(BF).reshape(12, 48, D)
        cp = pltpu.make_async_copy(ob.at[t], out.at[l, pl.ds(r, 12)], osem.at[t])
        cp.start()
        outs.append(cp)

    for cp in pend + halos + backs:
        cp.wait_send()
    for cp in outs:
        cp.wait()


def body(fields, region, gain_attn, w_qkv, w_proj, gain_mlp, w_up, w_down):
    down = w_down.T.reshape(4, 4, D).transpose(1, 0, 2).reshape(16, D)
    shard = jnp.stack([jnp.concatenate([w_qkv.T, w_proj.T], axis=0), w_up.T, down])
    tok = jnp.arange(WTOK, dtype=jnp.int32)
    toks = jnp.stack([(tok // WLON) % WLAT, tok % WLON]).reshape(2, WTOK, 1)
    vm = pl.BlockSpec(memory_space=pltpu.VMEM)
    hbm = pl.BlockSpec(memory_space=pl.ANY)
    dma = pltpu.SemaphoreType.DMA
    out = pl.pallas_call(
        kernel,
        out_shape=jax.ShapeDtypeStruct((2, 24, 48, D), BF),
        in_specs=[hbm, hbm, hbm, vm, vm, vm],
        out_specs=hbm,
        scratch_shapes=[
            pltpu.VMEM((3, 2, 2, 4, 2, 4, 16, D), BF),
            pltpu.VMEM((2, 27, 56, D), BF),
            pltpu.VMEM((2, 48, 48), jnp.int32),
            pltpu.VMEM((3 * D, D), BF),
            pltpu.VMEM((D, D), BF),
            pltpu.VMEM((D, FF), BF),
            pltpu.VMEM((576, D), BF),
            pltpu.VMEM((2304, D), BF),
            pltpu.VMEM((2304, D), BF),
            pltpu.VMEM((16, D, WTOK), BF),
            pltpu.VMEM((D, 128), BF),
            pltpu.VMEM((576, D), BF),
            pltpu.VMEM((2, 27, 56, D), BF),
            pltpu.VMEM((2, 24, 8, D), BF),
            pltpu.VMEM((4, WTOK, 128), BF),
            pltpu.VMEM((128, 256), BF),
            pltpu.VMEM((256, 128), F32),
            pltpu.VMEM((4, 12, 48, D), BF),
            dma((3, S_ALL)),
            dma((3, S_ALL)),
            dma((5,)),
            dma((9,)),
            dma((9,)),
            dma((4,)),
        ],
        compiler_params=pltpu.CompilerParams(
            collective_id=0, has_side_effects=True, vmem_limit_bytes=66 * 2**20 - 2**21
        ),
        name="block",
    )(shard, fields[0], region, gain_attn.reshape(1, D), gain_mlp.reshape(1, D), toks)
    return out[None]


def solution(mesh):
    in_specs = (
        P("mem", None, "lat", "lon", None),
        P("lat", "lon"),
        P(),
        P(None, ("mem", "lat", "lon")),
        P(None, ("mem", "lat", "lon")),
        P(),
        P(None, ("mem", "lat", "lon")),
        P(None, ("mem", "lat", "lon")),
    )
    out_specs = P("mem", None, "lat", "lon", None)
    return jax.shard_map(body, mesh=mesh, in_specs=in_specs, out_specs=out_specs, check_vma=False)
```

time: 652 us -> 141 us (0.22); the launches traced: 644 us -> 141 us
  waiting for transfers between devices: 295 us -> 0 us
  local copies, waits for them, and re-layouts: 201 us -> 4.77 us
  Pallas kernels: 0 us -> 134 us
  matrix products: 100 us -> 0 us
  starting transfers between devices: 18.8 us -> 0 us
  between operations: 14.2 us -> 0.02 us
  other arithmetic: 14.9 us -> 2.11 us
    all_gather x1 -> x0, waiting for transfers between devices: 277 us -> none  [one_gather(): lines, at, gathered = (lax.all_gather(flat, axis), 0, [])]
    pallas_call x0 -> x1, Pallas kernels: none -> 134 us  [body(): pl.pallas_call(kernel, out_shape=jax.ShapeDtypeStruct((2, 24, 48, D), BF)...]
    dot_general x5 -> x0, matrix products: 80.3 us -> none  [the longest x1 45.8 us: body(): pre_act = jnp.dot(normed2, gathered[2], preferred_element_type=jnp.float32)]
    reshape x10 -> x1, local copies, waits for them, and re-layouts: 56 us -> 0.81 us  [body(): toks = jnp.stack([tok // WLON % WLAT, tok % WLON]).reshape(2, WTOK, 1)]
    unnamed x31 -> x1, local copies, waits for them, and re-layouts: 42.4 us -> 3.23 us
    slice x14 -> x0, local copies, waits for them, and re-layouts: 36.8 us -> none  [the longest x1 24 us: attend(): windowed[:, :, 2]]
    transpose x8 -> x0, local copies, waits for them, and re-layouts: 29.1 us -> none  [the longest x4 13.2 us: in_order(): pieces = jnp.moveaxis(pieces, 0, dim)]
    sub x1 -> x0, matrix products: 19.9 us -> none  [attend(): attn_probs = jax.nn.softmax(scores, axis=-1).astype(jnp.bfloat16)]
  transfers between devices with their start and end apart: 7 -> 0, of which waited for: 5 -> 0; matrix products, arithmetic and copies ran while one was open for 5% -> 0% of each run, Pallas kernels for 0% -> 0%
where the time goes in v1:
time: 141 us
  Pallas kernels  134 us (95%)
  local copies, waits for them, and re-layouts  4.77 us (3%)
  other arithmetic  2.11 us (1%)
    pallas_call x1, Pallas kernels, body(): pl.pallas_call(kernel, out_shape=jax.ShapeDtypeStruct((2, 24, 48, D), BF)...  134 us
    unnamed x1, local copies, waits for them, and re-layouts  3.23 us

profile of v1, /device:TPU:1, one launch (start us, length us, event | category | flops | bytes accessed | tf_op | source)
XLA Modules:
  0.0 140.8 jit_solution(719110922063407158)
XLA Ops:
  0.0 0.7 maximum_bitcast_fusion
  0.8 0.7 stack_reshape.3
  1.5 1.3 pad_maximum_fusion.shard
  2.9 0.8 copy.11.toks
  3.7 133.9 %block.1 = bf16[2,24,48,512]{3,2,1,0:T(8,128)(2,1)} custom-call(bf16[3,16,512]{2,1,0:T(8,128)(2,1)} %pad_maximum_fusion.shard, bf16[2,24,48,512]{3,2,1,0:T(8,128)(2,1)} %bitcast.19, s32[24,48]{1,0:T(8,128)} %region.1, f32[1,512]{1,0:T(1,128)} %bitcast.24, f32[1,512]{1,0:T(1,128)} %bitcast.25, s32[2,144,1]{2,1,0:T(8,128)} %copy.11.toks), custom_call_target="tpu_custom_call" | custom-call | tf_op jit(solution)/shard_map/block/pallas_call | solution.py:398
  137.6 3.2 %copy.13 = bf16[1,2,24,48,512]{4,3,2,1,0:T(8,128)(2,1)} copy(bf16[1,2,24,48,512]{4,3,2,1,0:T(8,128)(2,1)} %bitcast.18) | data formatting | bytes 4718592
  (2 shorter events, 0.0 us)

commit v2 on v1

--- a/solution.py
+++ b/solution.py
@@ -65,14 +65,16 @@
     xb,
     q_s,
     k_s,
-    vt_s,
-    mt,
+    v_s,
+    bm,
+    bt,
     mix,
     ox,
     ic,
     km_mask,
     tq_mask,
     to_mask,
+    om_mask,
     ob,
     send,
     recv,
@@ -216,9 +218,10 @@
     tr = lax.broadcasted_iota(jnp.int32, (128, 256), 0)
     tl = lax.broadcasted_iota(jnp.int32, (128, 256), 1)
     tq_mask[...] = jnp.where((tr >> 4) == (tl >> 5), 1.0, 0.0).astype(BF)
-    tr = lax.broadcasted_iota(jnp.int32, (256, 128), 0)
-    tl = lax.broadcasted_iota(jnp.int32, (256, 128), 1)
-    to_mask[...] = jnp.where((tr >> 5) == (tl >> 4), 1.0, 0.0)
+    to_mask[...] = jnp.where((tr >> 4) == (tl >> 5), 1.0, 0.0)
+    tr = lax.broadcasted_iota(jnp.int32, (512, 128), 0)
+    tl = lax.broadcasted_iota(jnp.int32, (512, 128), 1)
+    om_mask[...] = jnp.where((tr >> 7) == (tl >> 5), 1.0, 0.0)
 
     is_up = core == 0
     for i in range(4):
@@ -282,64 +285,68 @@
             q_s[rows, cols] = (q * QSCALE).astype(BF)
             k = nt(xb[...], w_qkv[512 + 256 * n : 512 + 256 * n + 256, :])
             k_s[rows, cols] = k.astype(BF)
+            v = nt(xb[...], w_qkv[1024 + 256 * n : 1024 + 256 * n + 256, :])
+            v_s[rows, cols] = v.astype(BF)
+    @pl.loop(0, 4)
+    def _(b):
         for w in range(4):
-            vt = nt(w_qkv[1024:1536, :], xb[WTOK * w : WTOK * w + WTOK, :])
-            vt_s[b * 4 + w] = vt.astype(BF)
+            win = b * 4 + w
+            row = toks[0] + (6 * b + SH)
+            col = toks[1] + (WLON * w + SL)
+            l48 = lax.broadcasted_iota(jnp.int32, (WTOK, 48), 1)
+            sel = jnp.where(l48 == row, 1.0, 0.0).astype(BF)
+            near = nn(sel, reg[0].astype(F32).astype(BF))
+            far = nn(sel, reg[1].astype(F32).astype(BF))
+            ids = jnp.sum(
+                jnp.where(l48 == col, near, 0.0) + jnp.where(l48 + 48 == col, far, 0.0),
+                axis=1,
+                keepdims=True,
+            )
+            glob = lat * 24 + row
+            glob = jnp.where(glob >= NLAT_ALL, glob - NLAT_ALL, glob)
+            code = ids * 2.0 + jnp.where(glob < SH, 1.0, 0.0)
+            hot = jnp.where(code == lane.astype(F32), 1.0, 0.0).astype(BF)
+            bm[win] = (nt(hot, hot[0:128]) - 1.0) * (-NEG)
+            bt[win] = (nt(hot, jnp.concatenate([hot[128:144]] * 8, axis=0)) - 1.0) * (-NEG)
 
     def window(b, w):
         win = b * 4 + w
-        rows = pl.ds(pl.multiple_of(win * WTOK, 16), WTOK)
-        row = toks[0] + (6 * b + SH)
-        col = toks[1] + (WLON * w + SL)
-        l48 = lax.broadcasted_iota(jnp.int32, (WTOK, 48), 1)
-        sel = jnp.where(l48 == row, 1.0, 0.0).astype(BF)
-        near = nn(sel, reg[0].astype(F32).astype(BF))
-        far = nn(sel, reg[1].astype(F32).astype(BF))
-        ids = jnp.sum(
-            jnp.where(l48 == col, near, 0.0) + jnp.where(l48 + 48 == col, far, 0.0),
-            axis=1,
-            keepdims=True,
-        )
-        glob = lat * 24 + row
-        glob = jnp.where(glob >= NLAT_ALL, glob - NLAT_ALL, glob)
-        code = ids * 2.0 + jnp.where(glob < SH, 1.0, 0.0)
-        hot = jnp.where(code == lane.astype(F32), 1.0, 0.0).astype(BF)
-        bias_m = (nt(hot, hot[0:128]) - 1.0) * (-NEG)
-        bias_t = (nt(hot, jnp.concatenate([hot[128:144]] * 8, axis=0)) - 1.0) * (-NEG)
+        at0 = pl.multiple_of(win * WTOK, 16)
+        rows = pl.ds(at0, WTOK)
 
         def softmax(s):
-            m = jnp.max(s, axis=0, keepdims=True)
-            e = jnp.exp2(s - m)
-            return e.astype(BF), 1.0 / jnp.sum(e, axis=0, keepdims=True)
-
+            e = jnp.exp2(s - jnp.max(s, axis=-2, keepdims=True))
+            return (e * (1.0 / jnp.sum(e, axis=-2, keepdims=True))).astype(BF)
+
+        for s in range(4):
+            at = 128 * s
+            k4 = k_s[rows, at : at + 128]
+            q4 = q_s[pl.ds(at0, 128), at : at + 128]
+            sc = nt(jnp.concatenate([k4 * km_mask[h] for h in range(4)], axis=0), q4)
+            p = softmax(sc.reshape(4, WTOK, 128) + bm[win])
+            p = jnp.concatenate([p[h].T for h in range(4)], axis=0)
+            o = nn(p, v_s[rows, at : at + 128]) * om_mask[...]
+            o = o[0:128] + o[128:256] + o[256:384] + o[384:512]
+            mix[pl.ds(pl.multiple_of(w * WTOK, 16), 128), at : at + 128] = o.astype(BF)
         for g in range(2):
-            for s in range(2):
-                at = 256 * g + 128 * s
-                k4 = k_s[rows, at : at + 128]
-                q4 = q_s[pl.ds(pl.multiple_of(win * WTOK, 16), 128), at : at + 128]
-                for h in range(4):
-                    e, inv = softmax(nt(k4 * km_mask[h], q4) + bias_m)
-                    o = nn(vt_s[win, at + 32 * h : at + 32 * h + 32, :], e)
-                    mt[at + 32 * h : at + 32 * h + 32, :] = (o * inv).astype(BF)
             at = 256 * g
-            qt = q_s[pl.ds(pl.multiple_of(win * WTOK + 128, 16), 16), at : at + 256]
+            qt = q_s[pl.ds(pl.multiple_of(at0 + 128, 16), 16), at : at + 256]
             qt = jnp.concatenate([qt] * 8, axis=0) * tq_mask[...]
-            e, inv = softmax(nt(k_s[rows, at : at + 256], qt) + bias_t)
-            o = nn(vt_s[win, at : at + 256, :], e)
-            o = (o * inv * to_mask[...]).astype(BF).T
+            p = softmax(nt(k_s[rows, at : at + 256], qt) + bt[win]).T
+            o = nn(p, v_s[rows, at : at + 256]) * to_mask[...]
             acc = o[0:16]
             for h in range(1, 8):
                 acc = acc + o[16 * h : 16 * h + 16]
-            mix[pl.ds(pl.multiple_of(w * WTOK + 128, 16), 16), at : at + 256] = acc
-        mix[pl.ds(pl.multiple_of(w * WTOK, 16), 128), :] = mt[...].T
+            mix[pl.ds(pl.multiple_of(w * WTOK + 128, 16), 16), at : at + 256] = acc.astype(BF)
 
     zeros = jnp.zeros((8, D), BF)
 
     @pl.loop(0, 4)
     def _(b):
-        @pl.loop(0, 4)
+        @pl.loop(0, 2)
         def _(w):
-            window(b, w)
+            window(b, 2 * w)
+            window(b, 2 * w + 1)
 
         ao = nt(mix[...], w_p[...]).astype(BF)
         for l in range(2):
@@ -410,14 +417,16 @@
             pltpu.VMEM((576, D), BF),
             pltpu.VMEM((2304, D), BF),
             pltpu.VMEM((2304, D), BF),
-            pltpu.VMEM((16, D, WTOK), BF),
-            pltpu.VMEM((D, 128), BF),
+            pltpu.VMEM((2304, D), BF),
+            pltpu.VMEM((16, WTOK, 128), F32),
+            pltpu.VMEM((16, WTOK, 128), F32),
             pltpu.VMEM((576, D), BF),
             pltpu.VMEM((2, 27, 56, D), BF),
             pltpu.VMEM((2, 24, 8, D), BF),
             pltpu.VMEM((4, WTOK, 128), BF),
             pltpu.VMEM((128, 256), BF),
-            pltpu.VMEM((256, 128), F32),
+            pltpu.VMEM((128, 256), F32),
+            pltpu.VMEM((512, 128), F32),
             pltpu.VMEM((4, 12, 48, D), BF),
             dma((3, S_ALL)),
             dma((3, S_ALL)),

time: 141 us -> 110 us (0.78)
  Pallas kernels: 134 us -> 102 us
    pallas_call x1, Pallas kernels: 134 us -> 102 us  [body(): pl.pallas_call(kernel, out_shape=jax.ShapeDtypeStruct((2, 24, 48, D), BF)...]
where the time goes in v2:
time: 110 us; the launch traced here: 109 us
  Pallas kernels  102 us (93%)
  local copies, waits for them, and re-layouts  4.77 us (4%)
  other arithmetic  2.11 us (2%)
    pallas_call x1, Pallas kernels, body(): pl.pallas_call(kernel, out_shape=jax.ShapeDtypeStruct((2, 24, 48, D), BF)...  102 us
    unnamed x1, local copies, waits for them, and re-layouts  3.23 us

profile of v2, /device:TPU:1, one launch (start us, length us, event | category | flops | bytes accessed | tf_op | source)
XLA Modules:
  0.0 109.4 jit_solution(14683897445838686398)
XLA Ops:
  0.0 0.7 maximum_bitcast_fusion
  0.8 0.7 stack_reshape.3
  1.5 1.3 %pad_maximum_fusion.shard = bf16[3,16,512]{2,1,0:T(8,128)(2,1)} fusion(bf16[1,16,512]{2,1,0:T(8,128)(2,1)S(1)} %stack_reshape.3, bf16[1,16,512]{2,1,0:T(8,128)(2,1)} %bitcast.22, bf16[1,16,512]{2,1,0:T(8,128)(2,1)S(1)} %maximum_bitcast_fusion), kind=kLoop, calls=%fused_computation | loop fusion | flops 49152 | bytes 98304 | tf_op jit(solution)/shard_map/stack | solution.py:399
  2.9 0.8 copy.11.toks
  3.7 102.5 %block.1 = bf16[2,24,48,512]{3,2,1,0:T(8,128)(2,1)} custom-call(bf16[3,16,512]{2,1,0:T(8,128)(2,1)} %pad_maximum_fusion.shard, bf16[2,24,48,512]{3,2,1,0:T(8,128)(2,1)} %bitcast.19, s32[24,48]{1,0:T(8,128)} %region.1, f32[1,512]{1,0:T(1,128)} %bitcast.24, f32[1,512]{1,0:T(1,128)} %bitcast.25, s32[2,144,1]{2,1,0:T(8,128)} %copy.11.toks), custom_call_target="tpu_custom_call" | custom-call | tf_op jit(solution)/shard_map/block/pallas_call | solution.py:405
  106.1 3.2 %copy.13 = bf16[1,2,24,48,512]{4,3,2,1,0:T(8,128)(2,1)} copy(bf16[1,2,24,48,512]{4,3,2,1,0:T(8,128)(2,1)} %bitcast.18) | data formatting | bytes 4718592
  (2 shorter events, 0.0 us)

commit v3 on v2

v3 whole, which is shorter than its diff:
```python
import functools

import jax
import jax.numpy as jnp
from jax import lax
from jax.experimental import pallas as pl
from jax.experimental.pallas import tpu as pltpu
from jax.sharding import PartitionSpec as P

D = 512
FF = 2048
HDIM = 32
WLAT = 6
WLON = 12
WTOK = 144
SH = 3
SL = 6
NLAT_ALL = 96
QSCALE = 1.4426950408889634 / HDIM**0.5
NEG = -1e30
EPS = 1e-05
MESH = pl.DeviceIdType.MESH
BF = jnp.bfloat16
F32 = jnp.float32

UNITS = (
    (0, 0, (0, 2, 1)),
    (0, 1, (0, 1, 2)),
    (1, 0, (1, 2, 0)),
    (1, 1, (2, 1, 0)),
    (2, 0, (2, 0, 1)),
    (2, 1, (1, 0, 2)),
)
FIRST, LATER = (0, 1), (2, 3, 4, 5)


def nt(a, b):
    return lax.dot_general(a, b, (((1,), (1,)), ((), ())), preferred_element_type=F32)


def nn(a, b):
    return lax.dot_general(a, b, (((1,), (0,)), ((), ())), preferred_element_type=F32)


def norm(x, gain):
    x = x.astype(F32)
    mean = jnp.mean(x, axis=-1, keepdims=True)
    cen = x - mean
    var = jnp.mean(cen * cen, axis=-1, keepdims=True)
    return (cen * lax.rsqrt(var + EPS) * gain).astype(BF)


def kernel(
    w_qkv_in,
    w_p_in,
    w_u_in,
    w_d_in,
    fields,
    region,
    gain_a,
    gain_m,
    out,
    gat,
    fx,
    reg,
    w_qkv,
    w_p,
    w_d,
    xw,
    xb,
    q_s,
    k_s,
    v_s,
    bm,
    bt,
    mix,
    ox,
    ic,
    km_mask,
    tq_mask,
    to_mask,
    om_mask,
    ob,
    send,
    recv,
    loc,
    hsend,
    hrecv,
    bsend,
    brecv,
    osem,
):
    mem = lax.axis_index("mem")
    lat = lax.axis_index("lat")
    lon = lax.axis_index("lon")
    core = mem % 2
    y_lo = mem // 2
    y_hi = lon // 4
    x0 = lon % 4
    y0 = y_hi * 2 + y_lo
    pos = (x0, y0, lat)

    def dev(x, y, z, c):
        return ((y % 2) * 2 + c, z, (y // 2) * 4 + x)

    def moved(axis, dist, c=None):
        p = list(pos)
        p[axis] = (p[axis] + dist) % 4
        return dev(*p, core if c is None else c)

    sibling = dev(*pos, 1 - core)
    lat_b, lat_f = (lat + 3) % 4, (lat + 1) % 4
    lon_b, lon_f = (lon + 7) % 8, (lon + 1) % 8

    bar = pltpu.get_barrier_semaphore()
    peers = [moved(a, d) for a in range(3) for d in (1, 2, 3)] + [sibling]
    peers += [(mem, lat, lon_b), (mem, lat, lon_f), (mem, lat_b, lon_b), (mem, lat_f, lon_f)]
    for d in peers:
        pl.semaphore_signal(bar, inc=1, device_id=d, device_id_type=MESH)

    own = pltpu.make_async_copy(fields, fx.at[:, pl.ds(0, 24), pl.ds(0, 48)], loc.at[0])
    own.start()
    own_reg = pltpu.make_async_copy(region, reg.at[0, pl.ds(0, 24)], loc.at[1])
    own_reg.start()

    here = (y_lo, core, lat, y_hi, x0)
    gat[(0, *here)] = jnp.concatenate([w_qkv_in[...], w_p_in[...]], axis=0)
    gat[(1, *here)] = w_u_in[...]
    gat[(2, *here)] = jnp.concatenate(
        [w_d_in[:, 512 * k : 512 * k + 512] for k in range(4)], axis=0
    )

    def remote(src, dst, s, r, d):
        return pltpu.make_async_remote_copy(
            src_ref=src, dst_ref=dst, send_sem=s, recv_sem=r, device_id=d, device_id_type=MESH
        )

    def block(u, free, at=None):
        p, h, _ = UNITS[u]
        at = at or pos
        x = pl.ds(0, 4) if 0 in free else at[0]
        yl, yh = (pl.ds(0, 2), pl.ds(0, 2)) if 1 in free else (at[1] % 2, at[1] // 2)
        z = pl.ds(0, 4) if 2 in free else at[2]
        return gat.at[p, yl, core, z, yh, x, pl.ds(8 * h, 8)]

    steps = {}
    for u, (_, _, order) in enumerate(UNITS):
        for ph in range(3):
            r = block(u, order[:ph])
            for i, d in enumerate((1, 3, 2)):
                k = 3 * ph + i
                steps[u, ph, i] = remote(
                    r, r, send.at[u, k], recv.at[u, k], moved(order[ph], d)
                )
        for i, d in enumerate((0, 1, 3, 2)):
            at = list(pos)
            at[order[2]] = (at[order[2]] + 4 - d) % 4
            r = block(u, order[:2], at)
            steps[u, 3, i] = remote(r, r, send.at[u, 9 + i], recv.at[u, 9 + i], sibling)

    def start(units, ph, slots=(0, 1, 2)):
        for i in slots:
            for u in units:
                steps[u, ph, i].start()

    def arrived(units, ph, slots=(0, 1, 2)):
        for i in slots:
            for u in units:
                steps[u, ph, i].wait_recv()

    fsl = (
        (fields.at[:, :, pl.ds(0, 8)], fx.at[:, pl.ds(0, 24), pl.ds(48, 8)], (mem, lat, lon_b)),
        (fields.at[:, pl.ds(0, 3)], fx.at[:, pl.ds(24, 3), pl.ds(0, 48)], (mem, lat_b, lon)),
        (
            fields.at[:, pl.ds(0, 3), pl.ds(0, 8)],
            fx.at[:, pl.ds(24, 3), pl.ds(48, 8)],
            (mem, lat_b, lon_b),
        ),
        (region, reg.at[0, pl.ds(24, 24)], (mem, lat_b, lon)),
        (region, reg.at[1, pl.ds(0, 24)], (mem, lat, lon_b)),
        (region, reg.at[1, pl.ds(24, 24)], (mem, lat_b, lon_b)),
    )
    halos = [remote(s, t, hsend.at[i], hrecv.at[i], d) for i, (s, t, d) in enumerate(fsl)]

    def slab(b):
        rr = pl.ds(6 * b + SH, WLAT)
        return remote(
            ox.at[:, rr, pl.ds(48, 8)], ic.at[:, rr], bsend.at[b], brecv.at[b], (mem, lat, lon_f)
        )

    bsl = (
        (ox.at[:, pl.ds(24, 3), pl.ds(0, 48)], ox.at[:, pl.ds(0, 3), pl.ds(0, 48)], (mem, lat_f, lon)),
        (ox.at[:, pl.ds(24, 3), pl.ds(48, 8)], ic.at[:, pl.ds(0, 3)], (mem, lat_f, lon_f)),
    )
    backs = [
        remote(s, t, bsend.at[4 + i], brecv.at[4 + i], d) for i, (s, t, d) in enumerate(bsl)
    ]

    pl.semaphore_wait(bar, len(peers))
    start(FIRST, 0)
    for i in (3, 4, 5, 0):
        halos[i].start()
    start(LATER, 0)

    lane = lax.broadcasted_iota(jnp.int32, (WTOK, 128), 1)
    for h in range(4):
        km_mask[h] = jnp.where((lane >> 5) == h, 1.0, 0.0).astype(BF)
    tr = lax.broadcasted_iota(jnp.int32, (128, 256), 0)
    tl = lax.broadcasted_iota(jnp.int32, (128, 256), 1)
    tq_mask[...] = jnp.where((tr >> 4) == (tl >> 5), 1.0, 0.0).astype(BF)
    to_mask[...] = jnp.where((tr >> 4) == (tl >> 5), 1.0, 0.0)
    tr = lax.broadcasted_iota(jnp.int32, (512, 128), 0)
    tl = lax.broadcasted_iota(jnp.int32, (512, 128), 1)
    om_mask[...] = jnp.where((tr >> 7) == (tl >> 5), 1.0, 0.0)

    def cut(b, w):
        pieces = [
            fx[l, 6 * b + SH + i, WLON * w + SL : WLON * w + SL + WLON, :]
            for l in range(2)
            for i in range(WLAT)
        ]
        rows = pl.ds(pl.multiple_of((b * 4 + w) * WTOK, 16), WTOK)
        xw[rows, :] = norm(jnp.concatenate(pieces, axis=0), gain_a[...])

    arrived(FIRST, 0)
    start(FIRST, 1)
    own.wait()

    @pl.loop(0, 3)
    def _(b):
        for w in range(3):
            cut(b, w)

    arrived(FIRST, 1)
    start(FIRST, 2)
    start(FIRST, 3, (0,))
    for i in (1, 2):
        halos[i].start()
    arrived(LATER, 0)
    start(LATER, 1)

    own_reg.wait()
    for i in (3, 4, 5):
        halos[i].wait_recv()
    tok = lax.broadcasted_iota(jnp.int32, (WTOK, 1), 0)
    tok = jnp.where(tok >= 72, tok - 72, tok)
    tok_i = sum(jnp.where(tok >= 12 * k, 1, 0) for k in range(1, WLAT))
    tok_j = tok - 12 * tok_i

    @pl.loop(0, 4)
    def _(b):
        for w in range(4):
            win = b * 4 + w
            row = tok_i + (6 * b + SH)
            col = tok_j + (WLON * w + SL)
            l48 = lax.broadcasted_iota(jnp.int32, (WTOK, 48), 1)
            sel = jnp.where(l48 == row, 1.0, 0.0).astype(BF)
            near = nn(sel, reg[0].astype(F32).astype(BF))
            far = nn(sel, reg[1].astype(F32).astype(BF))
            ids = jnp.sum(
                jnp.where(l48 == col, near, 0.0) + jnp.where(l48 + 48 == col, far, 0.0),
                axis=1,
                keepdims=True,
            )
            glob = lat * 24 + row
            glob = jnp.where(glob >= NLAT_ALL, glob - NLAT_ALL, glob)
            code = ids * 2.0 + jnp.where(glob < SH, 1.0, 0.0)
            hot = jnp.where(code == lane.astype(F32), 1.0, 0.0).astype(BF)
            bm[win] = (nt(hot, hot[0:128]) - 1.0) * (-NEG)
            bt[win] = (nt(hot, jnp.concatenate([hot[128:144]] * 8, axis=0)) - 1.0) * (-NEG)

    halos[0].wait_recv()

    @pl.loop(0, 3)
    def _(b):
        cut(b, 3)

    for i in range(3):
        arrived(FIRST, 2, (i,))
        start(FIRST, 3, (i + 1,))
    arrived(FIRST, 3, (0, 1, 2, 3))

    @pl.loop(0, 32)
    def _(g):
        at = (g // 16, (g // 8) % 2, (g // 2) % 4, g % 2)
        v = gat[(0, *at)]
        w_qkv[pl.ds(pl.multiple_of(g * 48, 16), 48), :] = jnp.concatenate(
            [v[i, 0:12] for i in range(4)], axis=0
        )
        w_p[pl.ds(pl.multiple_of(g * 16, 16), 16), :] = jnp.concatenate(
            [v[i, 12:16] for i in range(4)], axis=0
        )

    @pl.loop(0, 4)
    def _(b):
        @pl.when(b == 1)
        def _():
            arrived(LATER, 1)
            start(LATER, 2)
            start(LATER, 3, (0,))

        @pl.when(b == 3)
        def _():
            halos[1].wait_recv()
            halos[2].wait_recv()
            for w in range(4):
                cut(3, w)

        rows = pl.ds(pl.multiple_of(b * 576, 16), 576)
        for n in range(2):
            cols = slice(256 * n, 256 * n + 256)
            q = nt(xw[rows, :], w_qkv[256 * n : 256 * n + 256, :])
            q_s[rows, cols] = (q * QSCALE).astype(BF)
            k = nt(xw[rows, :], w_qkv[512 + 256 * n : 512 + 256 * n + 256, :])
            k_s[rows, cols] = k.astype(BF)
            v = nt(xw[rows, :], w_qkv[1024 + 256 * n : 1024 + 256 * n + 256, :])
            v_s[rows, cols] = v.astype(BF)

    def window(b, w):
        win = b * 4 + w
        at0 = pl.multiple_of(win * WTOK, 16)
        rows = pl.ds(at0, WTOK)

        def softmax(s):
            e = jnp.exp2(s - jnp.max(s, axis=-2, keepdims=True))
            return (e * (1.0 / jnp.sum(e, axis=-2, keepdims=True))).astype(BF)

        for s in range(4):
            at = 128 * s
            k4 = k_s[rows, at : at + 128]
            q4 = q_s[pl.ds(at0, 128), at : at + 128]
            sc = nt(jnp.concatenate([k4 * km_mask[h] for h in range(4)], axis=0), q4)
            p = softmax(sc.reshape(4, WTOK, 128) + bm[win])
            p = jnp.concatenate([p[h].T for h in range(4)], axis=0)
            o = nn(p, v_s[rows, at : at + 128]) * om_mask[...]
            o = o[0:128] + o[128:256] + o[256:384] + o[384:512]
            mix[pl.ds(pl.multiple_of(w * WTOK, 16), 128), at : at + 128] = o.astype(BF)
        for g in range(2):
            at = 256 * g
            qt = q_s[pl.ds(pl.multiple_of(at0 + 128, 16), 16), at : at + 256]
            qt = jnp.concatenate([qt] * 8, axis=0) * tq_mask[...]
            p = softmax(nt(k_s[rows, at : at + 256], qt) + bt[win]).T
            o = nn(p, v_s[rows, at : at + 256]) * to_mask[...]
            acc = o[0:16]
            for h in range(1, 8):
                acc = acc + o[16 * h : 16 * h + 16]
            mix[pl.ds(pl.multiple_of(w * WTOK + 128, 16), 16), at : at + 256] = acc.astype(BF)

    zeros = jnp.zeros((8, D), BF)

    @pl.loop(0, 4)
    def _(turn):
        b = (turn + 3) % 4

        @pl.loop(0, 2)
        def _(w):
            window(b, 2 * w)
            window(b, 2 * w + 1)

        ao = nt(mix[...], w_p[...]).astype(BF)
        for l in range(2):
            for i in range(WLAT):
                at = 72 * l + 12 * i
                pieces = [ao[WTOK * w + at : WTOK * w + at + 12] for w in range(4)]
                ox[l, 6 * b + SH + i] = jnp.concatenate(
                    [zeros[0:6], *pieces, zeros[0:2]], axis=0
                )
        slab(b).start()

        @pl.when(turn == 0)
        def _():
            for cp in backs:
                cp.start()

        @pl.when(turn == 1)
        def _():
            arrived(LATER, 2)
            start(LATER, 3, (1, 2, 3))

    arrived(LATER, 3, (0, 1, 2, 3))

    @pl.loop(0, 32)
    def _(g):
        u = gat[(2, g // 16, (g // 8) % 2, (g // 2) % 4, g % 2)]
        for k in range(4):
            w_d[pl.ds(pl.multiple_of(g * 16, 16), 16), 512 * k : 512 * k + 512] = jnp.concatenate(
                [u[i, 4 * k : 4 * k + 4] for i in range(4)], axis=0
            )

    first = lax.broadcasted_iota(jnp.int32, (12, 8, D), 1) < SL

    outs = []
    for t in range(4):
        l, r = t % 2, 12 * (t // 2)
        if t == 0:
            for cp in (*backs, slab(0), slab(1)):
                cp.wait_recv()
        if t == 2:
            for cp in (slab(3), slab(2)):
                cp.wait_recv()
        att = ox[l, r : r + 12, 0:48, :].astype(F32)
        head = jnp.where(first, ic[l, r : r + 12].astype(F32), att[:, 0:8])
        att = jnp.concatenate([head, att[:, 8:48]], axis=1)
        res = (fx[l, r : r + 12, 0:48, :].astype(F32) + att).astype(BF).reshape(576, D)
        xb[...] = norm(res, gain_m[...])
        acc = res.astype(F32)
        for k in range(4):
            pre = nt(xb[...], gat[1, k // 2, k % 2].reshape(512, D))
            hid = (0.5 * pre * (1.0 + lax.erf(pre * 0.7071067811865476))).astype(BF)
            acc = acc + nt(hid, w_d[:, 512 * k : 512 * k + 512])
        ob[t] = acc.astype(BF).reshape(12, 48, D)
        cp = pltpu.make_async_copy(ob.at[t], out.at[l, pl.ds(r, 12)], osem.at[t])
        cp.start()
        outs.append(cp)

    for cp in (*steps.values(), *halos, *backs, *(slab(b) for b in range(4))):
        cp.wait_send()
    for cp in outs:
        cp.wait()


def body(fields, region, gain_attn, w_qkv, w_proj, gain_mlp, w_up, w_down):
    vm = pl.BlockSpec(memory_space=pltpu.VMEM)
    hbm = pl.BlockSpec(memory_space=pl.ANY)
    dma = pltpu.SemaphoreType.DMA
    out = pl.pallas_call(
        kernel,
        out_shape=jax.ShapeDtypeStruct((2, 24, 48, D), BF),
        in_specs=[vm, vm, vm, vm, hbm, hbm, vm, vm],
        out_specs=hbm,
        scratch_shapes=[
            pltpu.VMEM((3, 2, 2, 4, 2, 4, 16, D), BF),
            pltpu.VMEM((2, 27, 56, D), BF),
            pltpu.VMEM((2, 48, 48), jnp.int32),
            pltpu.VMEM((3 * D, D), BF),
            pltpu.VMEM((D, D), BF),
            pltpu.VMEM((D, FF), BF),
            pltpu.VMEM((2304, D), BF),
            pltpu.VMEM((576, D), BF),
            pltpu.VMEM((2304, D), BF),
            pltpu.VMEM((2304, D), BF),
            pltpu.VMEM((2304, D), BF),
            pltpu.VMEM((16, WTOK, 128), F32),
            pltpu.VMEM((16, WTOK, 128), F32),
            pltpu.VMEM((576, D), BF),
            pltpu.VMEM((2, 27, 56, D), BF),
            pltpu.VMEM((2, 27, 8, D), BF),
            pltpu.VMEM((4, WTOK, 128), BF),
            pltpu.VMEM((128, 256), BF),
            pltpu.VMEM((128, 256), F32),
            pltpu.VMEM((512, 128), F32),
            pltpu.VMEM((4, 12, 48, D), BF),
            dma((6, 13)),
            dma((6, 13)),
            dma((2,)),
            dma((6,)),
            dma((6,)),
            dma((6,)),
            dma((6,)),
            dma((4,)),
        ],
        compiler_params=pltpu.CompilerParams(
            collective_id=0, has_side_effects=True, vmem_limit_bytes=66 * 2**20 - 2**21
        ),
        name="block",
    )(
        w_qkv.T,
        w_proj.T,
        w_up.T,
        w_down.T,
        fields[0],
        region,
        gain_attn.reshape(1, D),
        gain_mlp.reshape(1, D),
    )
    return out[None]


def solution(mesh):
    in_specs = (
        P("mem", None, "lat", "lon", None),
        P("lat", "lon"),
        P(),
        P(None, ("mem", "lat", "lon")),
        P(None, ("mem", "lat", "lon")),
        P(),
        P(None, ("mem", "lat", "lon")),
        P(None, ("mem", "lat", "lon")),
    )
    out_specs = P("mem", None, "lat", "lon", None)
    return jax.shard_map(body, mesh=mesh, in_specs=in_specs, out_specs=out_specs, check_vma=False)
```

time: 110 us -> 82.2 us (0.75)
  Pallas kernels: 102 us -> 78 us
  other arithmetic: 2.11 us -> 0 us
  local copies, waits for them, and re-layouts: 4.77 us -> 3.23 us
    pallas_call x1, Pallas kernels: 102 us -> 78 us  [body(): pl.pallas_call(kernel, out_shape=jax.ShapeDtypeStruct((2, 24, 48, D), BF)...]
    another operation x2 -> x0, other arithmetic: 2.08 us -> none  [body(): jnp.stack([jnp.concatenate([w_qkv.T, w_proj.T], axis=0), w_up.T, down])]
where the time goes in v3:
time: 82.2 us; the launch traced here: 81.2 us
  Pallas kernels  78 us (95%)
  local copies, waits for them, and re-layouts  3.23 us (4%)
    pallas_call x1, Pallas kernels, body(): pl.pallas_call(kernel, out_shape=jax.ShapeDtypeStruct((2, 24, 48, D), BF)...  78 us
    unnamed x1, local copies, waits for them, and re-layouts  3.23 us

profile of v3, /device:TPU:1, one launch (start us, length us, event | category | flops | bytes accessed | tf_op | source)
XLA Modules:
  0.0 81.2 jit_solution(17895721950534679377)
XLA Ops:
  0.0 78.0 %block.1 = bf16[2,24,48,512]{3,2,1,0:T(8,128)(2,1)} custom-call(bf16[12,512]{1,0:T(8,128)(2,1)} %bitcast.10, bf16[4,512]{1,0:T(4,128)(2,1)} %bitcast.13, bf16[16,512]{1,0:T(8,128)(2,1)} %bitcast.11, bf16[4,2048]{1,0:T(4,128)(2,1)} %bitcast.12, bf16[2,24,48,512]{3,2,1,0:T(8,128)(2,1)} %bitcast.9, s32[24,48]{1,0:T(8,128)} %region.1, f32[1,512]{1,0:T(1,128)} %bitcast.14, ...), custom_call_target="tpu_custom_call" | custom-call | tf_op jit(solution)/shard_map/block/pallas_call | solution.py:426
  78.0 3.2 %copy.10 = bf16[1,2,24,48,512]{4,3,2,1,0:T(8,128)(2,1)} copy(bf16[1,2,24,48,512]{4,3,2,1,0:T(8,128)(2,1)} %bitcast.8) | data formatting | bytes 4718592

commit v4 on v3

--- a/solution.py
+++ b/solution.py
@@ -25,7 +25,7 @@
 
 UNITS = (
     (0, 0, (0, 2, 1)),
-    (0, 1, (0, 1, 2)),
+    (0, 1, (1, 2, 0)),
     (1, 0, (1, 2, 0)),
     (1, 1, (2, 1, 0)),
     (2, 0, (2, 0, 1)),

time: 82.2 us -> 78.5 us (0.955); the launches traced: 81.2 us -> 78.3 us
  Pallas kernels: 78 us -> 75.1 us
    pallas_call x1, Pallas kernels: 78 us -> 75.1 us  [body(): pl.pallas_call(kernel, out_shape=jax.ShapeDtypeStruct((2, 24, 48, D), BF)...]
where the time goes in v4:
time: 78.5 us; the launch traced here: 78.3 us
  Pallas kernels  75.1 us (96%)
  local copies, waits for them, and re-layouts  3.23 us (4%)
    pallas_call x1, Pallas kernels, body(): pl.pallas_call(kernel, out_shape=jax.ShapeDtypeStruct((2, 24, 48, D), BF)...  75.1 us
    unnamed x1, local copies, waits for them, and re-layouts  3.23 us

profile of v4, /device:TPU:1, one launch (start us, length us, event | category | flops | bytes accessed | tf_op | source)
XLA Modules:
  0.0 78.3 jit_solution(15378687018461269519)
XLA Ops:
  0.0 75.1 %block.1 = bf16[2,24,48,512]{3,2,1,0:T(8,128)(2,1)} custom-call(bf16[12,512]{1,0:T(8,128)(2,1)} %bitcast.10, bf16[4,512]{1,0:T(4,128)(2,1)} %bitcast.13, bf16[16,512]{1,0:T(8,128)(2,1)} %bitcast.11, bf16[4,2048]{1,0:T(4,128)(2,1)} %bitcast.12, bf16[2,24,48,512]{3,2,1,0:T(8,128)(2,1)} %bitcast.9, s32[24,48]{1,0:T(8,128)} %region.1, f32[1,512]{1,0:T(1,128)} %bitcast.14, ...), custom_call_target="tpu_custom_call" | custom-call | tf_op jit(solution)/shard_map/block/pallas_call | solution.py:426
  75.1 3.2 %copy.10 = bf16[1,2,24,48,512]{4,3,2,1,0:T(8,128)(2,1)} copy(bf16[1,2,24,48,512]{4,3,2,1,0:T(8,128)(2,1)} %bitcast.8) | data formatting | bytes 4718592

commit v5 on v4

--- a/solution.py
+++ b/solution.py
@@ -387,29 +387,29 @@
                 [u[i, 4 * k : 4 * k + 4] for i in range(4)], axis=0
             )
 
-    first = lax.broadcasted_iota(jnp.int32, (12, 8, D), 1) < SL
+    first = lax.broadcasted_iota(jnp.int32, (2, 12, 8, D), 2) < SL
 
     outs = []
-    for t in range(4):
-        l, r = t % 2, 12 * (t // 2)
+    for t in range(2):
+        r = 12 * t
         if t == 0:
             for cp in (*backs, slab(0), slab(1)):
                 cp.wait_recv()
-        if t == 2:
+        if t == 1:
             for cp in (slab(3), slab(2)):
                 cp.wait_recv()
-        att = ox[l, r : r + 12, 0:48, :].astype(F32)
-        head = jnp.where(first, ic[l, r : r + 12].astype(F32), att[:, 0:8])
-        att = jnp.concatenate([head, att[:, 8:48]], axis=1)
-        res = (fx[l, r : r + 12, 0:48, :].astype(F32) + att).astype(BF).reshape(576, D)
+        att = ox[:, r : r + 12, 0:48, :].astype(F32)
+        head = jnp.where(first, ic[:, r : r + 12].astype(F32), att[:, :, 0:8])
+        att = jnp.concatenate([head, att[:, :, 8:48]], axis=2)
+        res = (fx[:, r : r + 12, 0:48, :].astype(F32) + att).astype(BF).reshape(1152, D)
         xb[...] = norm(res, gain_m[...])
         acc = res.astype(F32)
         for k in range(4):
             pre = nt(xb[...], gat[1, k // 2, k % 2].reshape(512, D))
             hid = (0.5 * pre * (1.0 + lax.erf(pre * 0.7071067811865476))).astype(BF)
             acc = acc + nt(hid, w_d[:, 512 * k : 512 * k + 512])
-        ob[t] = acc.astype(BF).reshape(12, 48, D)
-        cp = pltpu.make_async_copy(ob.at[t], out.at[l, pl.ds(r, 12)], osem.at[t])
+        ob[t] = acc.astype(BF).reshape(2, 12, 48, D)
+        cp = pltpu.make_async_copy(ob.at[t], out.at[:, pl.ds(r, 12)], osem.at[t])
         cp.start()
         outs.append(cp)
 
@@ -436,7 +436,7 @@
             pltpu.VMEM((D, D), BF),
             pltpu.VMEM((D, FF), BF),
             pltpu.VMEM((2304, D), BF),
-            pltpu.VMEM((576, D), BF),
+            pltpu.VMEM((1152, D), BF),
             pltpu.VMEM((2304, D), BF),
             pltpu.VMEM((2304, D), BF),
             pltpu.VMEM((2304, D), BF),
@@ -449,7 +449,7 @@
             pltpu.VMEM((128, 256), BF),
             pltpu.VMEM((128, 256), F32),
             pltpu.VMEM((512, 128), F32),
-            pltpu.VMEM((4, 12, 48, D), BF),
+            pltpu.VMEM((2, 2, 12, 48, D), BF),
             dma((6, 13)),
             dma((6, 13)),
             dma((2,)),

time: 78.5 us -> 79.2 us (level)
  no operation moved by 1% of the time
where the time goes in v5:
time: 79.2 us; the launch traced here: 79 us
  Pallas kernels  75.7 us (96%)
  local copies, waits for them, and re-layouts  3.23 us (4%)
    pallas_call x1, Pallas kernels, body(): pl.pallas_call(kernel, out_shape=jax.ShapeDtypeStruct((2, 24, 48, D), BF)...  75.7 us
    unnamed x1, local copies, waits for them, and re-layouts  3.23 us

profile of v5, /device:TPU:1, one launch (start us, length us, event | category | flops | bytes accessed | tf_op | source)
XLA Modules:
  0.0 79.0 jit_solution(8049242110821027443)
XLA Ops:
  0.0 75.7 %block.1 = bf16[2,24,48,512]{3,2,1,0:T(8,128)(2,1)} custom-call(bf16[12,512]{1,0:T(8,128)(2,1)} %bitcast.10, bf16[4,512]{1,0:T(4,128)(2,1)} %bitcast.13, bf16[16,512]{1,0:T(8,128)(2,1)} %bitcast.11, bf16[4,2048]{1,0:T(4,128)(2,1)} %bitcast.12, bf16[2,24,48,512]{3,2,1,0:T(8,128)(2,1)} %bitcast.9, s32[24,48]{1,0:T(8,128)} %region.1, f32[1,512]{1,0:T(1,128)} %bitcast.14, ...), custom_call_target="tpu_custom_call" | custom-call | tf_op jit(solution)/shard_map/block/pallas_call | solution.py:426
  75.7 3.2 %copy.10 = bf16[1,2,24,48,512]{4,3,2,1,0:T(8,128)(2,1)} copy(bf16[1,2,24,48,512]{4,3,2,1,0:T(8,128)(2,1)} %bitcast.8) | data formatting | bytes 4718592
